TPU v7x, 512 devices: a whole 4x8x8 slice. The times are simulated.
512 devices in a mesh: gx: 16 (over y_hi, x), gy: 32 (over y_lo, z, core).
Axes of the slice: x: 4, y: 8 (y_hi: 4, y_lo: 2; y = y_hi * 2 + y_lo), z: 8, core: 2. Of those that a mesh axis runs over, the one named last changes fastest.
Arguments:
- density: float32 [16, 1024, 4096], P(None, 'gx', 'gy'), may hold values from 0.1 to 1
- cotangent: float32 [16, 1024, 4096], P(None, 'gx', 'gy'), may hold values from -6 to 6
Outputs:
- printed: float32 [16, 1024, 4096], P(None, 'gx', 'gy')
- gradient: float32 [16, 1024, 4096], P(None, 'gx', 'gy')
All inputs are finite; a program needn't handle non-finite values.
Results may differ from a plain program's by a relative error of at most 0.0003.
Values sent between devices are 32-bit elements; how exact they have to be, the bound alone decides.
A program may use at most 64 MiB of HBM per device.

v0:
```python
import math

import jax
import jax.numpy as jnp
from jax import lax
from jax.sharding import PartitionSpec as P

power_p = 20.0
root_q = 20.0 + math.log(5.0) / math.log(0.1)
smooth_eps = 0.0001


def with_halo(block, sides, width):
    for axis, dim in sides:
        count = lax.axis_size(axis)
        forward = [(i, i + 1) for i in range(count - 1)]
        forward.append((count - 1, 0))
        backward = [(target, source) for source, target in forward]
        low = lax.ppermute(
            lax.slice_in_dim(block, block.shape[dim] - width, None, axis=dim), axis, forward
        )
        high = lax.ppermute(lax.slice_in_dim(block, 0, width, axis=dim), axis, backward)
        block = jnp.concatenate([low, block, high], axis=dim)
    return block


def cross(plane):
    return (
        plane[1:-1, 1:-1] + plane[2:, 1:-1] + plane[:-2, 1:-1] + plane[1:-1, 2:] + plane[1:-1, :-2]
    )


def trim(plane, cells):
    if cells == 0:
        return plane
    return plane[cells : plane.shape[0] - cells, cells : plane.shape[1] - cells]


def forward_block(dens_pad, prev_pad, first, depth):
    prev = prev_pad
    layers = []
    for step in range(depth):
        total = cross(prev**power_p)
        level = jnp.where(first + step == 0, jnp.float32(1.0), total ** (1.0 / root_q))
        plane = trim(dens_pad[step], step + 1)
        diff = plane - level
        printed_layer = 0.5 * (
            plane + level - jnp.sqrt(diff * diff + smooth_eps) + math.sqrt(smooth_eps)
        )
        layers.append(trim(printed_layer, depth - step - 1))
        prev = printed_layer
    return (jnp.stack(layers), prev)


def backward_block(grad_pad, dens_pad, print_pad, state_pad, first, depth):
    carried = state_pad
    grads = [None] * depth
    for step in range(depth):
        local = depth - 1 - step
        width = depth - 1 - step
        spread = cross(carried)
        here = trim(print_pad[local + 1], depth - width)
        adjoint = (
            trim(grad_pad[local], depth - width)
            + power_p / root_q * here ** (power_p - 1.0) * spread
        )
        under = trim(print_pad[local], depth - width - 1)
        total = cross(under**power_p)
        level = jnp.where(first + local == 0, jnp.float32(1.0), total ** (1.0 / root_q))
        diff = trim(dens_pad[local], depth - width) - level
        root = jnp.sqrt(diff * diff + smooth_eps)
        grads[local] = trim(adjoint * 0.5 * (1.0 - diff / root), width)
        carried = adjoint * 0.5 * (1.0 + diff / root) * level / total
    return (jnp.stack(grads), carried)


def shards(density, cotangent):
    depth = 8
    layers_all = density.shape[0]
    blocks = layers_all // depth
    plane_shape = density.shape[1:]
    ones_layer = jnp.ones(plane_shape, jnp.float32)
    dens_all, grad_all = (
        with_halo(density, (("gx", 1), ("gy", 2)), depth),
        with_halo(cotangent, (("gx", 1), ("gy", 2)), depth),
    )

    def forward_step(index, carry):
        printed_all, prev = carry
        first = index * depth
        dens_pad = lax.dynamic_slice_in_dim(dens_all, first, depth, 0)
        prev_pad = with_halo(prev[None], (("gx", 1), ("gy", 2)), depth)[0]
        block, last = forward_block(dens_pad, prev_pad, first, depth)
        printed_all = lax.dynamic_update_slice_in_dim(printed_all, block, first, 0)
        return (printed_all, last)

    printed, final_layer = lax.fori_loop(
        0, blocks, forward_step, (jnp.zeros_like(density), ones_layer)
    )
    print_ext = jnp.concatenate([ones_layer[None], printed], 0)
    print_all = with_halo(print_ext, (("gx", 1), ("gy", 2)), depth)

    def backward_step(index, carry):
        gradient_all, carried = carry
        first = (blocks - 1 - index) * depth
        grad_pad = lax.dynamic_slice_in_dim(grad_all, first, depth, 0)
        dens_pad = lax.dynamic_slice_in_dim(dens_all, first, depth, 0)
        print_pad = lax.dynamic_slice_in_dim(print_all, first, depth + 1, 0)
        state_pad = with_halo(carried[None], (("gx", 1), ("gy", 2)), depth)[0]
        block, carried_next = backward_block(grad_pad, dens_pad, print_pad, state_pad, first, depth)
        gradient_all = lax.dynamic_update_slice_in_dim(gradient_all, block, first, 0)
        return (gradient_all, carried_next)

    gradient, final_state = lax.fori_loop(
        0, blocks, backward_step, (jnp.zeros_like(density), jnp.zeros(plane_shape, jnp.float32))
    )
    return (printed, gradient)


def solution(mesh):
    placed = (P(None, "gx", "gy"), P(None, "gx", "gy"))
    return jax.shard_map(
        shards,
        mesh=mesh,
        in_specs=placed,
        out_specs=(P(None, "gx", "gy"), P(None, "gx", "gy")),
        check_vma=False,
    )
```

profile of v0, /device:TPU:22, one launch (start us, length us, event | category | flops | bytes accessed | tf_op | source)
XLA Modules:
  0.0 253.3 jit_solution(568779422428762060)
XLA Ops:
  1.5 5.6 %collective-permute-start.8 = (f32[16,8,128]{2,1,0:T(8,128)S(1)}, f32[16,8,128]{2,1,0:T(8,128)S(1)}, u32[]{:S(2)}, u32[]{:S(2)}) collective-permute-start(f32[16,8,128]{2,1,0:T(8,128)S(1)} %get-tuple-element.375), channel_id=1, source_target_pairs={{0,32},{32,64},{64,96},{96,128},{128,160},{160,192},{192,224},{224... | collective-permute-start | bytes 196616 | tf_op jit(solution)/shard_map/ppermute | solution.py:19
  10.6 8.1 %collective-permute-start.12 = (f32[16,8,128]{2,1,0:T(8,128)}, f32[16,8,128]{2,1,0:T(8,128)S(1)}, u32[]{:S(2)}, u32[]{:S(2)}) collective-permute-start(f32[16,8,128]{2,1,0:T(8,128)} %get-tuple-element.373), channel_id=1, source_target_pairs={{0,32},{32,64},{64,96},{96,128},{128,160},{160,192},{192,224},{224... | collective-permute-start | bytes 196616 | tf_op jit(solution)/shard_map/ppermute | solution.py:19
  25.7 9.7 %collective-permute-start.11 = (f32[16,80,8]{1,2,0:T(8,128)S(1)}, f32[16,80,8]{1,2,0:T(8,128)S(1)}, u32[]{:S(2)}, u32[]{:S(2)}) collective-permute-start(f32[16,80,8]{1,2,0:T(8,128)S(1)} %get-tuple-element.368), channel_id=1, source_target_pairs={{1,0},{2,1},{3,2},{4,3},{5,4},{6,5},{7,6},{8,7},{9,8},{10,9},{11,1... | collective-permute-start | bytes 122888 | tf_op jit(solution)/shard_map/ppermute | solution.py:22
  38.4 3.2 %pad_maximum_fusion.3 = f32[16,80,144]{1,2,0:T(8,128)} fusion(f32[16,80,8]{1,2,0:T(8,128)S(1)} %collective-permute-done.11, f32[16,8,128]{1,2,0:T(8,128)} %copy-done.18, f32[16,64,128]{1,2,0:T(8,128)S(1)} %copy.16, f32[16,8,128]{1,2,0:T(8,128)} %copy-done.17, f32[16,80,8]{1,2,0:T(8,128)S(1)} %collective-permute-done.10), kind=kLoop, calls=%fused_computation.294 | loop fusion | flops 737280 | bytes 1474560 | tf_op jit(solution)/shard_map/concatenate | solution.py:23
  44.3 58.7 %while.32 = (s32[]{:T(128)}, f32[16,64,128]{2,1,0:T(8,128)}, f32[64,128]{1,0:T(8,128)S(1)}, f32[16,80,144]{2,1,0:T(8,128)S(1)}, s32[]{:T(128)}, /*index=5*/s32[]...) while((s32[]{:T(128)}, f32[16,64,128]{2,1,0:T(8,128)}, ...), condition=%wide.region_1.2_spmd.clone, body=%wide.region_0.1_spmd.clone.sunk | while | flops 996957 | bytes 9431385 | solution.py:97
  46.3 8.1 %collective-permute-start.1 = (f32[1,8,128]{2,1,0:T(8,128)S(1)}, f32[1,8,128]{2,1,0:T(8,128)S(1)}, u32[]{:S(2)}, u32[]{:S(2)}) collective-permute-start(f32[1,8,128]{2,1,0:T(8,128)S(1)} %get-tuple-element.523), channel_id=1, source_target_pairs={{0,32},{32,64},{64,96},{96,128},{128,160},{160,192},{192,224},{224... | collective-permute-start | bytes 12296 | tf_op jit(solution)/shard_map/while/body/eval_jaxpr/ppermute | solution.py:19
  56.4 3.5 %collective-permute-start.2 = (f32[1,80,8]{2,1,0:T(8,128)}, f32[1,80,8]{2,1,0:T(8,128)}, u32[]{:S(2)}, u32[]{:S(2)}) collective-permute-start(f32[1,80,8]{2,1,0:T(8,128)} %get-tuple-element.524), channel_id=1, source_target_pairs={{1,0},{2,1},{3,2},{4,3},{5,4},{6,5},{7,6},{8,7},{9,8},{10,9},{11,1... | collective-permute-start | bytes 7688 | tf_op jit(solution)/shard_map/while/body/eval_jaxpr/ppermute | solution.py:22
  62.7 5.0 %collective-permute-done.3 = f32[1,80,8]{2,1,0:T(8,128)} collective-permute-done((f32[1,80,8]{2,1,0:T(8,128)}, f32[1,80,8]{2,1,0:T(8,128)}, u32[]{:S(2)}, u32[]{:S(2)}) %collective-permute-start.3) | collective-permute-done | bytes 2592 | tf_op jit(solution)/shard_map/while/body/eval_jaxpr/ppermute | solution.py:19
  76.4 8.1 %collective-permute-start.1 = (f32[1,8,128]{2,1,0:T(8,128)S(1)}, f32[1,8,128]{2,1,0:T(8,128)S(1)}, u32[]{:S(2)}, u32[]{:S(2)}) collective-permute-start(f32[1,8,128]{2,1,0:T(8,128)S(1)} %get-tuple-element.523), channel_id=1, source_target_pairs={{0,32},{32,64},{64,96},{96,128},{128,160},{160,192},{192,224},{224... | collective-permute-start | bytes 12296 | tf_op jit(solution)/shard_map/while/body/eval_jaxpr/ppermute | solution.py:19
  88.4 2.4 collective-permute-start.3
  91.7 4.5 %collective-permute-done.3 = f32[1,80,8]{2,1,0:T(8,128)} collective-permute-done((f32[1,80,8]{2,1,0:T(8,128)}, f32[1,80,8]{2,1,0:T(8,128)}, u32[]{:S(2)}, u32[]{:S(2)}) %collective-permute-start.3) | collective-permute-done | bytes 2592 | tf_op jit(solution)/shard_map/while/body/eval_jaxpr/ppermute | solution.py:19
  103.9 8.4 %collective-permute-start.16 = (f32[17,8,128]{2,1,0:T(8,128)S(1)}, f32[17,8,128]{2,1,0:T(8,128)S(1)}, u32[]{:S(2)}, u32[]{:S(2)}) collective-permute-start(f32[17,8,128]{2,1,0:T(8,128)S(1)} %get-tuple-element.371), channel_id=1, source_target_pairs={{0,32},{32,64},{64,96},{96,128},{128,160},{160,192},{192,224},{224... | collective-permute-start | bytes 208904 | tf_op jit(solution)/shard_map/ppermute | solution.py:19
  112.3 2.1 collective-permute-start.17
  117.9 5.8 %collective-permute-start.15 = (f32[16,80,8]{1,2,0:T(8,128)}, f32[16,80,8]{1,2,0:T(8,128)}, u32[]{:S(2)}, u32[]{:S(2)}) collective-permute-start(f32[16,80,8]{1,2,0:T(8,128)} %get-tuple-element.366), channel_id=1, source_target_pairs={{1,0},{2,1},{3,2},{4,3},{5,4},{6,5},{7,6},{8,7},{9,8},{10,9},{11,1... | collective-permute-start | bytes 122888 | tf_op jit(solution)/shard_map/ppermute | solution.py:22
  129.8 2.0 copy.23
  131.8 5.9 %collective-permute-start.19 = (f32[17,80,8]{1,2,0:T(8,128)}, f32[17,80,8]{1,2,0:T(8,128)}, u32[]{:S(2)}, u32[]{:S(2)}) collective-permute-start(f32[17,80,8]{1,2,0:T(8,128)} %copy.23), channel_id=1, source_target_pairs={{1,0},{2,1},{3,2},{4,3},{5,4},{6,5},{7,6},{8,7},{9,8},{10,9},{11,1... | collective-permute-start | bytes 130568 | tf_op jit(solution)/shard_map/ppermute | solution.py:22
  137.8 2.9 %pad_maximum_fusion.4 = f32[16,80,144]{1,2,0:T(8,128)} fusion(f32[16,80,8]{1,2,0:T(8,128)} %collective-permute-done.15, f32[16,8,128]{1,2,0:T(8,128)} %copy.21, f32[16,64,128]{1,2,0:T(8,128)S(1)} %copy.20, f32[16,8,128]{1,2,0:T(8,128)S(1)} %copy.19, f32[16,80,8]{1,2,0:T(8,128)} %collective-permute-done.14), kind=kLoop, calls=%fused_computation.295 | loop fusion | flops 737280 | bytes 1474560 | tf_op jit(solution)/shard_map/concatenate | solution.py:23
  140.7 2.1 copy.24
  142.7 2.0 copy.25
  147.5 105.8 %while.33 = (s32[]{:T(128)}, f32[16,64,128]{2,1,0:T(8,128)}, f32[64,128]{1,0:T(8,128)S(1)}, f32[16,80,144]{1,2,0:T(8,128)}, f32[17,80,144]{2,1,0:T(8,128)S(1)}, ...) while((s32[]{:T(128)}, f32[16,64,128]{2,1,0:T(8,128)}, ...), condition=%wide.region_3.4_spmd.clone, body=%wide.region_2.3_spmd.clone.sunk | while | flops 2203911 | bytes 23524856 | solution.py:114
  150.1 8.1 %collective-permute-start.5 = (f32[1,8,128]{2,1,0:T(8,128)}, f32[1,8,128]{2,1,0:T(8,128)S(1)}, u32[]{:S(2)}, u32[]{:S(2)}) collective-permute-start(f32[1,8,128]{2,1,0:T(8,128)} %get-tuple-element.580), channel_id=1, source_target_pairs={{0,32},{32,64},{64,96},{96,128},{128,160},{160,192},{192,224},{224... | collective-permute-start | bytes 12296 | tf_op jit(solution)/shard_map/while/body/eval_jaxpr/ppermute | solution.py:19
  170.4 2.6 %collective-permute-start.6 = (f32[1,80,8]{2,1,0:T(8,128)}, f32[1,80,8]{2,1,0:T(8,128)}, u32[]{:S(2)}, u32[]{:S(2)}) collective-permute-start(f32[1,80,8]{2,1,0:T(8,128)} %get-tuple-element.581), channel_id=1, source_target_pairs={{1,0},{2,1},{3,2},{4,3},{5,4},{6,5},{7,6},{8,7},{9,8},{10,9},{11,1... | collective-permute-start | bytes 7688 | tf_op jit(solution)/shard_map/while/body/eval_jaxpr/ppermute | solution.py:22
  201.6 8.1 %collective-permute-start.5 = (f32[1,8,128]{2,1,0:T(8,128)}, f32[1,8,128]{2,1,0:T(8,128)S(1)}, u32[]{:S(2)}, u32[]{:S(2)}) collective-permute-start(f32[1,8,128]{2,1,0:T(8,128)} %get-tuple-element.580), channel_id=1, source_target_pairs={{0,32},{32,64},{64,96},{96,128},{128,160},{160,192},{192,224},{224... | collective-permute-start | bytes 12296 | tf_op jit(solution)/shard_map/while/body/eval_jaxpr/ppermute | solution.py:19
  222.0 5.2 %collective-permute-start.6 = (f32[1,80,8]{2,1,0:T(8,128)}, f32[1,80,8]{2,1,0:T(8,128)}, u32[]{:S(2)}, u32[]{:S(2)}) collective-permute-start(f32[1,80,8]{2,1,0:T(8,128)} %get-tuple-element.581), channel_id=1, source_target_pairs={{1,0},{2,1},{3,2},{4,3},{5,4},{6,5},{7,6},{8,7},{9,8},{10,9},{11,1... | collective-permute-start | bytes 7688 | tf_op jit(solution)/shard_map/while/body/eval_jaxpr/ppermute | solution.py:22
  (366 shorter events, 137.4 us)
Async XLA Ops:
  1.5 20.5 %collective-permute-start.8 = (f32[16,8,128]{2,1,0:T(8,128)S(1)}, f32[16,8,128]{2,1,0:T(8,128)S(1)}, u32[]{:S(2)}, u32[]{:S(2)}) collective-permute-start(f32[16,8,128]{2,1,0:T(8,128)S(1)} %get-tuple-element.375), channel_id=1, source_target_pairs={{0,32},{32,64},{64,96},{96,128},{128,160},{160,192},{192,224},{224... | collective-permute-start | bytes 196616 | tf_op jit(solution)/shard_map/ppermute | solution.py:19
  7.1 15.3 %collective-permute-start.9 = (f32[16,8,128]{2,1,0:T(8,128)S(1)}, f32[16,8,128]{2,1,0:T(8,128)S(1)}, u32[]{:S(2)}, u32[]{:S(2)}) collective-permute-start(f32[16,8,128]{2,1,0:T(8,128)S(1)} %get-tuple-element.376), channel_id=1, source_target_pairs={{32,0},{64,32},{96,64},{128,96},{160,128},{192,160},{224,192},{256... | collective-permute-start | bytes 196616 | tf_op jit(solution)/shard_map/ppermute | solution.py:22
  10.6 26.2 %collective-permute-start.12 = (f32[16,8,128]{2,1,0:T(8,128)}, f32[16,8,128]{2,1,0:T(8,128)S(1)}, u32[]{:S(2)}, u32[]{:S(2)}) collective-permute-start(f32[16,8,128]{2,1,0:T(8,128)} %get-tuple-element.373), channel_id=1, source_target_pairs={{0,32},{32,64},{64,96},{96,128},{128,160},{160,192},{192,224},{224... | collective-permute-start | bytes 196616 | tf_op jit(solution)/shard_map/ppermute | solution.py:19
  18.7 18.4 %collective-permute-start.13 = (f32[16,8,128]{2,1,0:T(8,128)}, f32[16,8,128]{2,1,0:T(8,128)S(1)}, u32[]{:S(2)}, u32[]{:S(2)}) collective-permute-start(f32[16,8,128]{2,1,0:T(8,128)} %get-tuple-element.374), channel_id=1, source_target_pairs={{32,0},{64,32},{96,64},{128,96},{160,128},{192,160},{224,192},{256... | collective-permute-start | bytes 196616 | tf_op jit(solution)/shard_map/ppermute | solution.py:22
  23.8 14.7 %collective-permute-start.10 = (f32[16,80,8]{1,2,0:T(8,128)}, f32[16,80,8]{1,2,0:T(8,128)S(1)}, u32[]{:S(2)}, u32[]{:S(2)}) collective-permute-start(f32[16,80,8]{1,2,0:T(8,128)} %get-tuple-element.367), channel_id=1, source_target_pairs={{0,1},{1,2},{2,3},{3,4},{4,5},{5,6},{6,7},{7,8},{8,9},{9,10},{10,1... | collective-permute-start | bytes 122888 | tf_op jit(solution)/shard_map/ppermute | solution.py:19
  25.7 12.7 %collective-permute-start.11 = (f32[16,80,8]{1,2,0:T(8,128)S(1)}, f32[16,80,8]{1,2,0:T(8,128)S(1)}, u32[]{:S(2)}, u32[]{:S(2)}) collective-permute-start(f32[16,80,8]{1,2,0:T(8,128)S(1)} %get-tuple-element.368), channel_id=1, source_target_pairs={{1,0},{2,1},{3,2},{4,3},{5,4},{6,5},{7,6},{8,7},{9,8},{10,9},{11,1... | collective-permute-start | bytes 122888 | tf_op jit(solution)/shard_map/ppermute | solution.py:22
  44.3 10.1 %collective-permute-start = (f32[1,8,128]{2,1,0:T(8,128)S(1)}, f32[1,8,128]{2,1,0:T(8,128)S(1)}, u32[]{:S(2)}, u32[]{:S(2)}) collective-permute-start(f32[1,8,128]{2,1,0:T(8,128)S(1)} %get-tuple-element.522), channel_id=1, source_target_pairs={{32,0},{64,32},{96,64},{128,96},{160,128},{192,160},{224,192},{256... | collective-permute-start | bytes 12296 | tf_op jit(solution)/shard_map/while/body/eval_jaxpr/ppermute | solution.py:22
  46.3 9.5 %collective-permute-start.1 = (f32[1,8,128]{2,1,0:T(8,128)S(1)}, f32[1,8,128]{2,1,0:T(8,128)S(1)}, u32[]{:S(2)}, u32[]{:S(2)}) collective-permute-start(f32[1,8,128]{2,1,0:T(8,128)S(1)} %get-tuple-element.523), channel_id=1, source_target_pairs={{0,32},{32,64},{64,96},{96,128},{128,160},{160,192},{192,224},{224... | collective-permute-start | bytes 12296 | tf_op jit(solution)/shard_map/while/body/eval_jaxpr/ppermute | solution.py:19
  74.4 10.1 %collective-permute-start = (f32[1,8,128]{2,1,0:T(8,128)S(1)}, f32[1,8,128]{2,1,0:T(8,128)S(1)}, u32[]{:S(2)}, u32[]{:S(2)}) collective-permute-start(f32[1,8,128]{2,1,0:T(8,128)S(1)} %get-tuple-element.522), channel_id=1, source_target_pairs={{32,0},{64,32},{96,64},{128,96},{160,128},{192,160},{224,192},{256... | collective-permute-start | bytes 12296 | tf_op jit(solution)/shard_map/while/body/eval_jaxpr/ppermute | solution.py:22
  76.4 9.5 %collective-permute-start.1 = (f32[1,8,128]{2,1,0:T(8,128)S(1)}, f32[1,8,128]{2,1,0:T(8,128)S(1)}, u32[]{:S(2)}, u32[]{:S(2)}) collective-permute-start(f32[1,8,128]{2,1,0:T(8,128)S(1)} %get-tuple-element.523), channel_id=1, source_target_pairs={{0,32},{32,64},{64,96},{96,128},{128,160},{160,192},{192,224},{224... | collective-permute-start | bytes 12296 | tf_op jit(solution)/shard_map/while/body/eval_jaxpr/ppermute | solution.py:19
  103.9 19.9 %collective-permute-start.16 = (f32[17,8,128]{2,1,0:T(8,128)S(1)}, f32[17,8,128]{2,1,0:T(8,128)S(1)}, u32[]{:S(2)}, u32[]{:S(2)}) collective-permute-start(f32[17,8,128]{2,1,0:T(8,128)S(1)} %get-tuple-element.371), channel_id=1, source_target_pairs={{0,32},{32,64},{64,96},{96,128},{128,160},{160,192},{192,224},{224... | collective-permute-start | bytes 208904 | tf_op jit(solution)/shard_map/ppermute | solution.py:19
  112.3 11.5 %collective-permute-start.17 = (f32[17,8,128]{2,1,0:T(8,128)S(1)}, f32[17,8,128]{2,1,0:T(8,128)S(1)}, u32[]{:S(2)}, u32[]{:S(2)}) collective-permute-start(f32[17,8,128]{2,1,0:T(8,128)S(1)} %get-tuple-element.372), channel_id=1, source_target_pairs={{32,0},{64,32},{96,64},{128,96},{160,128},{192,160},{224,192},{256... | collective-permute-start | bytes 208904 | tf_op jit(solution)/shard_map/ppermute | solution.py:22
  116.0 21.7 %collective-permute-start.14 = (f32[16,80,8]{1,2,0:T(8,128)}, f32[16,80,8]{1,2,0:T(8,128)}, u32[]{:S(2)}, u32[]{:S(2)}) collective-permute-start(f32[16,80,8]{1,2,0:T(8,128)} %get-tuple-element.365), channel_id=1, source_target_pairs={{0,1},{1,2},{2,3},{3,4},{4,5},{5,6},{6,7},{7,8},{8,9},{9,10},{10,1... | collective-permute-start | bytes 122888 | tf_op jit(solution)/shard_map/ppermute | solution.py:19
  117.9 19.8 %collective-permute-start.15 = (f32[16,80,8]{1,2,0:T(8,128)}, f32[16,80,8]{1,2,0:T(8,128)}, u32[]{:S(2)}, u32[]{:S(2)}) collective-permute-start(f32[16,80,8]{1,2,0:T(8,128)} %get-tuple-element.366), channel_id=1, source_target_pairs={{1,0},{2,1},{3,2},{4,3},{5,4},{6,5},{7,6},{8,7},{9,8},{10,9},{11,1... | collective-permute-start | bytes 122888 | tf_op jit(solution)/shard_map/ppermute | solution.py:22
  127.9 12.7 %collective-permute-start.18 = (f32[17,80,8]{1,2,0:T(8,128)}, f32[17,80,8]{1,2,0:T(8,128)}, u32[]{:S(2)}, u32[]{:S(2)}) collective-permute-start(f32[17,80,8]{1,2,0:T(8,128)} %copy.22), channel_id=1, source_target_pairs={{0,1},{1,2},{2,3},{3,4},{4,5},{5,6},{6,7},{7,8},{8,9},{9,10},{10,1... | collective-permute-start | bytes 130568 | tf_op jit(solution)/shard_map/ppermute | solution.py:19
  131.8 10.9 %collective-permute-start.19 = (f32[17,80,8]{1,2,0:T(8,128)}, f32[17,80,8]{1,2,0:T(8,128)}, u32[]{:S(2)}, u32[]{:S(2)}) collective-permute-start(f32[17,80,8]{1,2,0:T(8,128)} %copy.23), channel_id=1, source_target_pairs={{1,0},{2,1},{3,2},{4,3},{5,4},{6,5},{7,6},{8,7},{9,8},{10,9},{11,1... | collective-permute-start | bytes 130568 | tf_op jit(solution)/shard_map/ppermute | solution.py:22
  148.1 21.5 %collective-permute-start.4 = (f32[1,8,128]{2,1,0:T(8,128)}, f32[1,8,128]{2,1,0:T(8,128)S(1)}, u32[]{:S(2)}, u32[]{:S(2)}) collective-permute-start(f32[1,8,128]{2,1,0:T(8,128)} %get-tuple-element.579), channel_id=1, source_target_pairs={{32,0},{64,32},{96,64},{128,96},{160,128},{192,160},{224,192},{256... | collective-permute-start | bytes 12296 | tf_op jit(solution)/shard_map/while/body/eval_jaxpr/ppermute | solution.py:22
  150.1 19.6 %collective-permute-start.5 = (f32[1,8,128]{2,1,0:T(8,128)}, f32[1,8,128]{2,1,0:T(8,128)S(1)}, u32[]{:S(2)}, u32[]{:S(2)}) collective-permute-start(f32[1,8,128]{2,1,0:T(8,128)} %get-tuple-element.580), channel_id=1, source_target_pairs={{0,32},{32,64},{64,96},{96,128},{128,160},{160,192},{192,224},{224... | collective-permute-start | bytes 12296 | tf_op jit(solution)/shard_map/while/body/eval_jaxpr/ppermute | solution.py:19
  170.4 14.9 %collective-permute-start.6 = (f32[1,80,8]{2,1,0:T(8,128)}, f32[1,80,8]{2,1,0:T(8,128)}, u32[]{:S(2)}, u32[]{:S(2)}) collective-permute-start(f32[1,80,8]{2,1,0:T(8,128)} %get-tuple-element.581), channel_id=1, source_target_pairs={{1,0},{2,1},{3,2},{4,3},{5,4},{6,5},{7,6},{8,7},{9,8},{10,9},{11,1... | collective-permute-start | bytes 7688 | tf_op jit(solution)/shard_map/while/body/eval_jaxpr/ppermute | solution.py:22
  172.9 12.3 %collective-permute-start.7 = (f32[1,80,8]{2,1,0:T(8,128)}, f32[1,80,8]{2,1,0:T(8,128)}, u32[]{:S(2)}, u32[]{:S(2)}) collective-permute-start(f32[1,80,8]{2,1,0:T(8,128)} %get-tuple-element.582), channel_id=1, source_target_pairs={{0,1},{1,2},{2,3},{3,4},{4,5},{5,6},{6,7},{7,8},{8,9},{9,10},{10,1... | collective-permute-start | bytes 7688 | tf_op jit(solution)/shard_map/while/body/eval_jaxpr/ppermute | solution.py:19
  199.7 21.5 %collective-permute-start.4 = (f32[1,8,128]{2,1,0:T(8,128)}, f32[1,8,128]{2,1,0:T(8,128)S(1)}, u32[]{:S(2)}, u32[]{:S(2)}) collective-permute-start(f32[1,8,128]{2,1,0:T(8,128)} %get-tuple-element.579), channel_id=1, source_target_pairs={{32,0},{64,32},{96,64},{128,96},{160,128},{192,160},{224,192},{256... | collective-permute-start | bytes 12296 | tf_op jit(solution)/shard_map/while/body/eval_jaxpr/ppermute | solution.py:22
  201.6 19.6 %collective-permute-start.5 = (f32[1,8,128]{2,1,0:T(8,128)}, f32[1,8,128]{2,1,0:T(8,128)S(1)}, u32[]{:S(2)}, u32[]{:S(2)}) collective-permute-start(f32[1,8,128]{2,1,0:T(8,128)} %get-tuple-element.580), channel_id=1, source_target_pairs={{0,32},{32,64},{64,96},{96,128},{128,160},{160,192},{192,224},{224... | collective-permute-start | bytes 12296 | tf_op jit(solution)/shard_map/while/body/eval_jaxpr/ppermute | solution.py:19
  222.0 17.5 %collective-permute-start.6 = (f32[1,80,8]{2,1,0:T(8,128)}, f32[1,80,8]{2,1,0:T(8,128)}, u32[]{:S(2)}, u32[]{:S(2)}) collective-permute-start(f32[1,80,8]{2,1,0:T(8,128)} %get-tuple-element.581), channel_id=1, source_target_pairs={{1,0},{2,1},{3,2},{4,3},{5,4},{6,5},{7,6},{8,7},{9,8},{10,9},{11,1... | collective-permute-start | bytes 7688 | tf_op jit(solution)/shard_map/while/body/eval_jaxpr/ppermute | solution.py:22
  227.1 12.3 %collective-permute-start.7 = (f32[1,80,8]{2,1,0:T(8,128)}, f32[1,80,8]{2,1,0:T(8,128)}, u32[]{:S(2)}, u32[]{:S(2)}) collective-permute-start(f32[1,80,8]{2,1,0:T(8,128)} %get-tuple-element.582), channel_id=1, source_target_pairs={{0,1},{1,2},{2,3},{3,4},{4,5},{5,6},{6,7},{7,8},{8,9},{9,10},{10,1... | collective-permute-start | bytes 7688 | tf_op jit(solution)/shard_map/while/body/eval_jaxpr/ppermute | solution.py:19
  (88 other events, 304.0 us)
where the time goes:
time: 257 us; the launch traced here: 253 us
  starting transfers between devices  117 us (46%)
  local copies, waits for them, and re-layouts  64.5 us (25%)
  other arithmetic  57.5 us (22%)
  waiting for transfers between devices  12.1 us (5%)
    ppermute x14, starting transfers between devices, with_halo(): lax.ppermute(lax.slice_in_dim(block, block.shape[dim] - width, None, axis...  68.6 us
    ppermute x14, starting transfers between devices, with_halo(): lax.ppermute(lax.slice_in_dim(block, 0, width, axis=dim), axis, backward)  48 us
    while x186, local copies, waits for them, and re-layouts  25.3 us
    div x30, other arithmetic, backward_block(): carried = adjoint * 0.5 * (1.0 + diff / root) * level / total  20.7 us
    ppermute x14, waiting for transfers between devices, with_halo(): lax.ppermute(lax.slice_in_dim(block, block.shape[dim] - width, None, axis...  12.1 us
    while x14, other arithmetic  11.8 us
    slice x13, local copies, waits for them, and re-layouts, with_halo(): lax.slice_in_dim(block, block.shape[dim] - width, None, axis=dim)  10.5 us
    pow x16, other arithmetic, forward_block(): total = cross(prev ** power_p)  8.59 us
  transfers between devices with their start and end apart: 28, of which 4 were waited for; matrix products, arithmetic and copies ran while one was open for 25% of the time, Pallas kernels for 0%

commit v1 on v0

v1 whole, which is shorter than its diff:
```python
import math

import jax
import jax.numpy as jnp
from jax import lax
from jax.experimental import pallas as pl
from jax.experimental.pallas import tpu as pltpu
from jax.sharding import PartitionSpec as P

power_p = 20.0
root_q = 20.0 + math.log(5.0) / math.log(0.1)
smooth_eps = 0.0001

NZ = 16
ROWS = 64
LANES = 128
WIDE = 32
NEAR = 16
F32 = jnp.float32
MESH = pl.DeviceIdType.MESH

REACH = [2 * (NZ - 1) - z for z in range(NZ)]


def up8(n):
    return (n + 7) // 8 * 8


def place(counts):
    out, vec, first, last, prev = [], 0, None, 0, 0
    for n in counts:
        if first is None:
            off, first = 0, n
        else:
            off = last + max(prev, n)
            if off > LANES - first or off + n > LANES:
                vec, off, first = vec + 1, 0, n
        out.append((vec, off))
        last, prev = off, n
    return out, vec + 1


def stream(order, width):
    starts, chunks, at, sent = {}, [], 0, 0
    for z in order:
        starts[z] = at
        at += width(z)
        end = up8(at)
        chunks.append((sent, end - sent))
        sent = end
    return starts, chunks, sent


class Plan:
    def __init__(self, order, width, merges):
        self.order, self.width = order, width
        self.starts, chunks, self.rows = stream(order, width)
        self.row_chunks, self.row_need, at = [], {}, 0
        for count in merges:
            part = chunks[at : at + count]
            for z in order[at : at + count]:
                self.row_need[z] = len(self.row_chunks)
            self.row_chunks.append((part[0][0], sum(n for _, n in part)))
            at += count
        places, self.col_vecs = place([width(z) for z in order])
        self.cols = {z: p for z, p in zip(order, places)}
        self.corners, base = {}, 0
        firsts = []
        for bands in ((0,), (1,), (2, 3)):
            items = [
                (z, b, width(z) - 8 * b - 1)
                for b in bands
                for z in order
                if width(z) - 8 * b - 1 > 0
            ]
            if not items:
                continue
            places, vecs = place([n for _, _, n in items])
            for (z, b, n), (vec, off) in zip(items, places):
                self.corners[(z, b)] = (base + vec, off, n)
            for vec in range(vecs):
                firsts.append(min(order.index(z) for (z, b, n), p in zip(items, places) if p[0] == vec))
            base += vecs
        rank = sorted(range(base), key=lambda v: firsts[v])
        where = {v: i for i, v in enumerate(rank)}
        self.corners = {k: (where[v], o, n) for k, (v, o, n) in self.corners.items()}
        self.corner_vecs = base
        self.corner_chunks, self.corner_first = [], []
        for i, v in enumerate(rank):
            if self.corner_first and firsts[v] == self.corner_first[-1]:
                at, n = self.corner_chunks[-1]
                self.corner_chunks[-1] = (at, n + 8)
            else:
                self.corner_chunks.append((8 * i, 8))
                self.corner_first.append(firsts[v])

    def corner_need(self, z):
        need = -1
        for (layer, _), (vec, _, _) in self.corners.items():
            if layer == z:
                for i, (at, n) in enumerate(self.corner_chunks):
                    if at <= 8 * vec < at + n:
                        need = max(need, i)
        return need


DENS = Plan(list(range(NZ)), lambda z: REACH[z], [1] * NZ)
COTS = Plan(list(range(NZ - 1, 0, -1)), lambda z: z, [1, 1, 2, 4, 7])
PLANS = (DENS, COTS)


def messages(plan):
    out, seen = [], set()
    for i, z in enumerate(plan.order):
        wanted = [("row", plan.row_need[z])]
        if plan.corner_need(z) >= 0:
            wanted += [("corner", c) for c in range(plan.corner_need(z) + 1)]
        wanted += [("col", plan.cols[z][0])]
        for m in wanted:
            if m not in seen:
                seen.add(m)
                out.append(m)
    return out


COPIES = [messages(plan) for plan in PLANS]
SLOTS = [[(kind, c) for kind, c in copies for _ in range(4 if kind == "corner" else 2)] for copies in COPIES]
N_SEMS = sum(len(s) for s in SLOTS)


def lane_ids(shape):
    return lax.broadcasted_iota(jnp.int32, shape, len(shape) - 1)


def rotate(x, shift, axis=None):
    shift = shift % LANES
    if shift == 0:
        return x
    return pltpu.roll(x, shift, x.ndim - 1 if axis is None else axis)


def cross(ref, lo, hi):
    here = ref[:, lo:hi, :]
    lane = lane_ids(here.shape)
    east = rotate(here, 1)
    west = rotate(here, LANES - 1)
    swap = lambda v: jnp.concatenate([v[1:], v[:1]], axis=0)
    return (
        here
        + ref[:, lo - 1 : hi - 1, :]
        + ref[:, lo + 1 : hi + 1, :]
        + jnp.where(lane == 0, swap(east), east)
        + jnp.where(lane == LANES - 1, swap(west), west)
    )


def spans(margin, halo):
    out = []
    if halo:
        out.append((margin - halo, margin))
    out += [(margin, margin + ROWS // 2), (margin + ROWS // 2, margin + ROWS)]
    if halo:
        out.append((margin + ROWS, margin + ROWS + halo))
    return out


def kernel(
    dens_hbm,
    cots_hbm,
    printed_ref,
    grad_ref,
    dens,
    cots,
    t_even,
    t_odd,
    k_even,
    k_odd,
    coef,
    weight,
    shrink,
    row_out_d,
    row_in_d,
    col_out_d,
    col_in_d,
    cor_out_d,
    cor_in_d,
    row_out_c,
    row_in_c,
    col_out_c,
    col_in_c,
    cor_out_c,
    cor_in_c,
    load_sem,
    send_sem,
    recv_sem,
):
    gx, gy = lax.axis_index("gx"), lax.axis_index("gy")
    nx, ny = lax.axis_size("gx"), lax.axis_size("gy")
    up, down = lax.rem(gx + nx - 1, nx), lax.rem(gx + 1, nx)
    left, right = lax.rem(gy + ny - 1, ny), lax.rem(gy + 1, ny)

    load_d = pltpu.make_async_copy(dens_hbm, dens.at[:, 0, WIDE : WIDE + ROWS], load_sem.at[0])
    load_c = pltpu.make_async_copy(cots_hbm, cots.at[:, 0, NEAR : NEAR + ROWS], load_sem.at[1])
    load_d.start()
    load_c.start()

    barrier = pltpu.get_barrier_semaphore()
    for x, y in (
        (up, gy), (down, gy), (gx, left), (gx, right),
        (up, left), (up, right), (down, left), (down, right),
    ):
        pl.semaphore_signal(barrier, inc=1, device_id={"gx": x, "gy": y}, device_id_type=MESH)

    bufs = (
        (dens, WIDE, (row_out_d, col_out_d, cor_out_d), (row_in_d, col_in_d, cor_in_d)),
        (cots, NEAR, (row_out_c, col_out_c, cor_out_c), (row_in_c, col_in_c, cor_in_c)),
    )

    def pack(which):
        plan = PLANS[which]
        src, margin, (row, col, cor), _ = bufs[which]
        for z in plan.order:
            w, at = plan.width(z), plan.starts[z]
            row[0, at : at + w, :] = src[z, 0, margin : margin + w, :]
            row[1, at : at + w, :] = src[z, 0, margin + ROWS - w : margin + ROWS, :]
        for vec in range(plan.col_vecs):
            lane = lane_ids((ROWS, LANES))
            low = high = None
            for z in plan.order:
                v, off = plan.cols[z]
                if v != vec:
                    continue
                w = plan.width(z)
                turned = rotate(src[z, 0, margin : margin + ROWS, :], off)
                if low is None:
                    low = high = turned
                else:
                    low = jnp.where(lane >= off, turned, low)
                    high = jnp.where((lane >= off - w) & (lane < off), turned, high)
            col[0, vec * ROWS : (vec + 1) * ROWS, :] = low
            col[1, vec * ROWS : (vec + 1) * ROWS, :] = high
        lane = lane_ids((8, LANES))
        for vec in range(plan.corner_vecs):
            for side in range(2):
                low = high = None
                for (z, b), (v, off, n) in plan.corners.items():
                    if v != vec:
                        continue
                    lo = margin + 8 * b if side == 0 else margin + ROWS - 8 * (b + 1)
                    turned = rotate(src[z, 0, lo : lo + 8, :], off)
                    if low is None:
                        low = high = turned
                    else:
                        low = jnp.where(lane >= off, turned, low)
                        high = jnp.where((lane >= off - n) & (lane < off), turned, high)
                cor[2 * side, 8 * vec : 8 * vec + 8, :] = low
                cor[2 * side + 1, 8 * vec : 8 * vec + 8, :] = high

    copies = ({}, {})
    count = 0
    for which, plan in enumerate(PLANS):
        _, _, outs, ins = bufs[which]
        for kind, c in COPIES[which]:
            made = []
            if kind == "row":
                at, n = plan.row_chunks[c]
                targets = [(0, up, gy), (1, down, gy)]
                src, dst = outs[0], ins[0]
            elif kind == "col":
                at, n = c * ROWS, ROWS
                targets = [(0, gx, left), (1, gx, right)]
                src, dst = outs[1], ins[1]
            else:
                at, n = plan.corner_chunks[c]
                targets = [(0, up, left), (1, up, right), (2, down, left), (3, down, right)]
                src, dst = outs[2], ins[2]
            for i, x, y in targets:
                made.append(
                    pltpu.make_async_remote_copy(
                        src_ref=src.at[i, at : at + n],
                        dst_ref=dst.at[i, at : at + n],
                        send_sem=send_sem.at[count],
                        recv_sem=recv_sem.at[count],
                        device_id={"gx": x, "gy": y},
                        device_id_type=MESH,
                    )
                )
                count += 1
            copies[which][(kind, c)] = made

    load_d.wait()
    pack(0)
    load_c.wait()
    pack(1)
    pl.semaphore_wait(barrier, 8)
    for which in range(2):
        for m in COPIES[which]:
            for copy in copies[which][m]:
                copy.start()

    arrived = (set(), set())

    def receive(which, z):
        plan = PLANS[which]
        dst, margin, _, (row, col, cor) = bufs[which]
        wanted = [("row", c) for c in range(plan.row_need[z] + 1)]
        wanted += [("corner", c) for c in range(plan.corner_need(z) + 1)]
        wanted += [("col", c) for c in range(plan.cols[z][0] + 1)]
        for m in wanted:
            if m not in arrived[which]:
                arrived[which].add(m)
                for copy in copies[which][m]:
                    copy.wait_recv()
        w, at = plan.width(z), plan.starts[z]
        dst[z, 0, margin + ROWS : margin + ROWS + w, :] = row[0, at : at + w, :]
        dst[z, 0, margin - w : margin, :] = row[1, at : at + w, :]
        vec, off = plan.cols[z]
        lane = lane_ids((ROWS, LANES))
        part = slice(vec * ROWS, (vec + 1) * ROWS)
        both = jnp.where((lane >= off) & (lane < off + w), col[0, part, :], col[1, part, :])
        dst[z, 1, margin : margin + ROWS, :] = rotate(both, LANES - off)
        lane = lane_ids((8, LANES))
        for b in range(4):
            if (z, b) not in plan.corners:
                continue
            vec, off, n = plan.corners[(z, b)]
            part = slice(8 * vec, 8 * vec + 8)
            slot = (lane >= off) & (lane < off + n)
            low = jnp.where(slot, cor[0, part, :], cor[1, part, :])
            high = jnp.where(slot, cor[2, part, :], cor[3, part, :])
            lo = margin + ROWS + 8 * b
            dst[z, 1, lo : lo + 8, :] = rotate(low, LANES - off)
            lo = margin - 8 * (b + 1)
            dst[z, 1, lo : lo + 8, :] = rotate(high, LANES - off)

    towers = (t_even, t_odd)
    inner = WIDE - NEAR
    for z in range(NZ):
        receive(0, z)
        below, above = towers[(z + 1) % 2], towers[z % 2]
        for lo, hi in spans(WIDE, up8(REACH[z])):
            plane = dens[z, :, lo:hi, :]
            if z == 0:
                level = jnp.ones_like(plane)
            else:
                total = cross(below, lo + 8, hi + 8)
                logs = jnp.log(total)
                level = jnp.exp(logs * (1.0 / root_q))
            diff = plane - level
            square = diff * diff + smooth_eps
            inverse = lax.rsqrt(square)
            layer = 0.5 * (plane + level - square * inverse) + 0.5 * math.sqrt(smooth_eps)
            p2 = layer * layer
            p4 = p2 * p2
            p8 = p4 * p4
            p16 = p8 * p8
            p19 = p16 * (p2 * layer)
            if z < NZ - 1:
                above[:, lo + 8 : hi + 8, :] = p19 * layer
            near_lo, near_hi = max(lo, WIDE - up8(z)), min(hi, WIDE + ROWS + up8(z))
            if near_lo < near_hi:
                cut = lambda v: v[:, near_lo - lo : near_hi - lo, :]
                tilt = 0.5 * (cut(diff) * cut(inverse))
                coef[z, :, near_lo - inner : near_hi - inner, :] = (power_p / root_q) * cut(p19)
                if z > 0:
                    weight[z, :, near_lo - inner : near_hi - inner, :] = (0.5 + tilt) * jnp.exp(
                        cut(logs) * (1.0 / root_q - 1.0)
                    )
                if WIDE <= lo and hi <= WIDE + ROWS:
                    printed_ref[z, lo - WIDE : hi - WIDE, :] = layer[0]
                    shrink[z, lo - WIDE : hi - WIDE, :] = 0.5 - tilt[0]

    carried = (k_even, k_odd)
    for z in reversed(range(NZ)):
        if z > 0:
            receive(1, z)
        above, here = carried[(z + 1) % 2], carried[z % 2]
        for lo, hi in spans(NEAR, up8(z)):
            if z == 0:
                adjoint = cots[z, 0, lo:hi, :] + coef[z, 0, lo:hi, :] * cross(above, lo + 8, hi + 8)[0]
            elif z == NZ - 1:
                adjoint = cots[z, :, lo:hi, :]
            else:
                adjoint = cots[z, :, lo:hi, :] + coef[z, :, lo:hi, :] * cross(above, lo + 8, hi + 8)
            if z > 0:
                here[:, lo + 8 : hi + 8, :] = adjoint * weight[z, :, lo:hi, :]
            if NEAR <= lo and hi <= NEAR + ROWS:
                own = adjoint if z == 0 else adjoint[0]
                rows = slice(lo - NEAR, hi - NEAR)
                grad_ref[z, rows, :] = own * shrink[z, rows, :]

    for which in range(2):
        for m in COPIES[which]:
            for copy in copies[which][m]:
                copy.wait_send()


def shards(density, cotangent):
    def packed(plan):
        out = []
        for shape in ((2, plan.rows, LANES), (2, plan.col_vecs * ROWS, LANES), (4, 8 * plan.corner_vecs, LANES)):
            out += [pltpu.VMEM(shape, F32)] * 2
        return out

    wide, near = 2 * WIDE + ROWS, 2 * NEAR + ROWS
    shape = jax.ShapeDtypeStruct(density.shape, F32)
    return pl.pallas_call(
        kernel,
        out_shape=(shape, shape),
        in_specs=[pl.BlockSpec(memory_space=pl.ANY)] * 2,
        out_specs=(pl.BlockSpec(memory_space=pltpu.VMEM),) * 2,
        scratch_shapes=[
            pltpu.VMEM((NZ, 2, wide, LANES), F32),
            pltpu.VMEM((NZ, 2, near, LANES), F32),
            pltpu.VMEM((2, wide + 16, LANES), F32),
            pltpu.VMEM((2, wide + 16, LANES), F32),
            pltpu.VMEM((2, near + 16, LANES), F32),
            pltpu.VMEM((2, near + 16, LANES), F32),
            pltpu.VMEM((NZ, 2, near, LANES), F32),
            pltpu.VMEM((NZ, 2, near, LANES), F32),
            pltpu.VMEM((NZ, ROWS, LANES), F32),
            *packed(DENS),
            *packed(COTS),
            pltpu.SemaphoreType.DMA((2,)),
            pltpu.SemaphoreType.DMA((N_SEMS,)),
            pltpu.SemaphoreType.DMA((N_SEMS,)),
        ],
        compiler_params=pltpu.CompilerParams(collective_id=0, has_side_effects=True),
    )(density, cotangent)


def solution(mesh):
    placed = (P(None, "gx", "gy"), P(None, "gx", "gy"))
    return jax.shard_map(
        shards,
        mesh=mesh,
        in_specs=placed,
        out_specs=placed,
        check_vma=False,
    )
```

time: 257 us -> 39.8 us (0.15)
  the two profiles are of different devices: /device:TPU:22 before, /device:TPU:8 now
where the time goes in v1:
time: 39.8 us; the launch traced here: 39.7 us
  Pallas kernels  36.3 us (91%)
  local copies, waits for them, and re-layouts  2.74 us (7%)
  between operations  0.65 us (2%)
    pallas_call x1, Pallas kernels, shards(): pl.pallas_call(kernel, out_shape=(shape, shape), in_specs=[pl.BlockSpec(m...  36.3 us
    unnamed x4, local copies, waits for them, and re-layouts  2.74 us

profile of v1, /device:TPU:8, one launch (start us, length us, event | category | flops | bytes accessed | tf_op | source)
XLA Modules:
  0.0 39.7 jit_solution(8280260945078534805)
XLA Ops:
  0.6 36.3 %shard_map.41 = (f32[16,64,128]{2,1,0:T(8,128)}, f32[16,64,128]{2,1,0:T(8,128)}) custom-call(f32[16,64,128]{2,1,0:T(8,128)} %dens_hbm.1, f32[16,64,128]{2,1,0:T(8,128)} %cots_hbm.1), custom_call_target="tpu_custom_call" | custom-call | tf_op jit(solution)/shard_map/pallas_call | solution.py:407
  36.9 0.0 copy-start
  36.9 1.9 %copy.6 = f32[16,64,128]{2,1,0:T(8,128)} copy(f32[16,64,128]{2,1,0:T(8,128)} %get-tuple-element.4) | data formatting | bytes 1048576
  38.9 0.0 copy-done
  38.9 0.8 %copy.7 = f32[16,64,128]{2,1,0:T(8,128)} copy(f32[16,64,128]{2,1,0:T(8,128)S(1)} %copy-done) | data formatting | bytes 1048576
Async XLA Ops:
  36.9 2.0 %copy-start = (f32[16,64,128]{2,1,0:T(8,128)S(1)}, f32[16,64,128]{2,1,0:T(8,128)}, u32[]{:S(2)}) copy-start(f32[16,64,128]{2,1,0:T(8,128)} %get-tuple-element.5) | copy-start | bytes 1572868

commit v2 on v1

--- a/solution.py
+++ b/solution.py
@@ -104,17 +104,19 @@
         return need
 
 
-DENS = Plan(list(range(NZ)), lambda z: REACH[z], [1] * NZ)
+DENS = Plan(list(range(NZ)), lambda z: REACH[z], [1] * 8 + [2] * 4)
 COTS = Plan(list(range(NZ - 1, 0, -1)), lambda z: z, [1, 1, 2, 4, 7])
 PLANS = (DENS, COTS)
+
+RELAYED = [(0, 8), (0, 9), (0, 10), (0, 11), (1, 0), (1, 1), (1, 2), (1, 3), (1, 4)]
+PASS_ON = {1: [4], 2: [5], 3: [6], 4: [7], 5: [8]}
 
 
 def messages(plan):
     out, seen = [], set()
     for i, z in enumerate(plan.order):
-        wanted = [("row", plan.row_need[z])]
-        if plan.corner_need(z) >= 0:
-            wanted += [("corner", c) for c in range(plan.corner_need(z) + 1)]
+        wanted = [("corner", c) for c in range(len(plan.corner_chunks))]
+        wanted += [("row", plan.row_need[z])]
         wanted += [("col", plan.cols[z][0])]
         for m in wanted:
             if m not in seen:
@@ -126,6 +128,20 @@
 COPIES = [messages(plan) for plan in PLANS]
 SLOTS = [[(kind, c) for kind, c in copies for _ in range(4 if kind == "corner" else 2)] for copies in COPIES]
 N_SEMS = sum(len(s) for s in SLOTS)
+
+
+OPPOSITE = (1, 0, 3, 2, 7, 6, 5, 4, 9, 8, 10)
+URGENT = (7, 5, 3)
+TOKEN_ORDER = (3, 1, 10, 7, 0, 8, 9, 5, 2, 6, 4)
+
+
+def rank(gx, gy):
+    x, y = lax.rem(gx, 4), 2 * lax.div(gx, 4) + lax.div(gy, 16)
+    z, core = lax.rem(lax.div(gy, 2), 8), lax.rem(gy, 2)
+    far = lax.div(y, 4)
+    hops = y * (1 - 2 * far) + 8 * far
+    first = 1 - lax.div(gx * 32 + gy + 511, 512)
+    return 13 * z + 8 * hops + 9 * x + 4 * (1 - core) + 60 * first
 
 
 def lane_ids(shape):
@@ -178,6 +194,8 @@
     coef,
     weight,
     shrink,
+    relay_d,
+    relay_c,
     row_out_d,
     row_in_d,
     col_out_d,
@@ -193,6 +211,9 @@
     load_sem,
     send_sem,
     recv_sem,
+    token_sem,
+    relay_send,
+    relay_recv,
 ):
     gx, gy = lax.axis_index("gx"), lax.axis_index("gy")
     nx, ny = lax.axis_size("gx"), lax.axis_size("gy")
@@ -204,12 +225,43 @@
     load_d.start()
     load_c.start()
 
-    barrier = pltpu.get_barrier_semaphore()
-    for x, y in (
+    around = (
         (up, gy), (down, gy), (gx, left), (gx, right),
         (up, left), (up, right), (down, left), (down, right),
-    ):
-        pl.semaphore_signal(barrier, inc=1, device_id={"gx": x, "gy": y}, device_id_type=MESH)
+        (lax.rem(gx + 4, nx), gy), (lax.rem(gx + nx - 4, nx), gy), (gx + 3 - 2 * lax.rem(gx, 4), gy),
+    )
+    mine = rank(gx, gy)
+    low_end, high_end = lax.rem(gx, 4) == 0, lax.rem(gx, 4) == 3
+    at_end = jnp.logical_or(low_end, high_end)
+    ends = (low_end, high_end, None, None, low_end, low_end, high_end, high_end)
+    later, ready, earlier, greets = [], [], [], []
+    for d, (x, y) in enumerate(around):
+        lag = rank(x, y) - mine
+        slack = 20 if d < 4 else 0 if d < 8 else 30
+        if d < 8 and ends[d] is not None:
+            slack = slack + (30 - slack) * ends[d].astype(jnp.int32)
+        later.append(lag > slack)
+        ready.append(lag <= slack)
+        mutual = jnp.logical_and(lag <= slack, lag >= -slack)
+        earlier.append(lag < -slack)
+        greets.append(jnp.logical_or(lag > slack, mutual))
+    for d in range(8, 11):
+        for flags in (later, ready, earlier, greets):
+            flags[d] = jnp.logical_and(at_end, flags[d])
+    barrier = pltpu.get_barrier_semaphore()
+    for d, (x, y) in enumerate(around):
+        pl.when(greets[d])(
+            lambda x=x, y=y: pl.semaphore_signal(
+                barrier, inc=1, device_id={"gx": x, "gy": y}, device_id_type=MESH
+            )
+        )
+    pl.semaphore_wait(barrier, sum(v.astype(jnp.int32) for v in ready))
+    for d, (x, y) in enumerate(around):
+        pl.when(earlier[d])(
+            lambda d=d, x=x, y=y: pl.semaphore_signal(
+                token_sem.at[OPPOSITE[d]], inc=1, device_id={"gx": x, "gy": y}, device_id_type=MESH
+            )
+        )
 
     bufs = (
         (dens, WIDE, (row_out_d, col_out_d, cor_out_d), (row_in_d, col_in_d, cor_in_d)),
@@ -256,7 +308,8 @@
                 cor[2 * side, 8 * vec : 8 * vec + 8, :] = low
                 cor[2 * side + 1, 8 * vec : 8 * vec + 8, :] = high
 
-    copies = ({}, {})
+    copies, order = ({}, {}), ([], [])
+    relays, hops, vias = (relay_d, relay_c), [[] for _ in RELAYED], {}
     count = 0
     for which, plan in enumerate(PLANS):
         _, _, outs, ins = bufs[which]
@@ -264,39 +317,112 @@
             made = []
             if kind == "row":
                 at, n = plan.row_chunks[c]
-                targets = [(0, up, gy), (1, down, gy)]
+                targets = [(0, 0), (1, 1)]
                 src, dst = outs[0], ins[0]
             elif kind == "col":
                 at, n = c * ROWS, ROWS
-                targets = [(0, gx, left), (1, gx, right)]
+                targets = [(0, 2), (1, 3)]
                 src, dst = outs[1], ins[1]
             else:
                 at, n = plan.corner_chunks[c]
-                targets = [(0, up, left), (1, up, right), (2, down, left), (3, down, right)]
+                targets = [(0, 4), (1, 5), (2, 6), (3, 7)]
                 src, dst = outs[2], ins[2]
-            for i, x, y in targets:
-                made.append(
+            for i, d in targets:
+                x, y = around[d]
+                copy = (
                     pltpu.make_async_remote_copy(
                         src_ref=src.at[i, at : at + n],
                         dst_ref=dst.at[i, at : at + n],
-                        send_sem=send_sem.at[count],
+                        send_sem=send_sem.at[8 * which + d],
                         recv_sem=recv_sem.at[count],
                         device_id={"gx": x, "gy": y},
                         device_id_type=MESH,
                     )
                 )
+                made.append(copy)
+                if (which, c) in RELAYED and kind == "row":
+                    k = RELAYED.index((which, c))
+                    end, beyond = ((low_end, 9), (high_end, 8))[i]
+                    x, y = around[10]
+                    via = pltpu.make_async_remote_copy(
+                        src_ref=src.at[i, at : at + n],
+                        dst_ref=relays[which].at[at : at + n],
+                        send_sem=send_sem.at[8 * which + d],
+                        recv_sem=relay_recv.at[k],
+                        device_id={"gx": x, "gy": y},
+                        device_id_type=MESH,
+                    )
+                    x, y = around[beyond]
+                    onward = pltpu.make_async_remote_copy(
+                        src_ref=relays[which].at[at : at + n],
+                        dst_ref=dst.at[i, at : at + n],
+                        send_sem=relay_send.at[which],
+                        recv_sem=recv_sem.at[count],
+                        device_id={"gx": x, "gy": y},
+                        device_id_type=MESH,
+                    )
+                    order[which].append((d, copy, jnp.logical_not(end)))
+                    order[which].append((10, via, end))
+                    hops[k].append(onward)
+                    vias[k] = via
+                else:
+                    order[which].append((d, copy, None))
                 count += 1
             copies[which][(kind, c)] = made
 
+    def sent(src, dst, sem):
+        pltpu.make_async_remote_copy(
+            src_ref=src,
+            dst_ref=dst,
+            send_sem=sem,
+            recv_sem=recv_sem.at[0],
+            device_id={"gx": up, "gy": gy},
+            device_id_type=MESH,
+        ).wait_send()
+
     load_d.wait()
     pack(0)
+
+    def send(which, d, gate):
+        for e, copy, on in order[which]:
+            if d is not None and e != d:
+                continue
+            conds = [v for v in (gate[e] if gate else None, on) if v is not None]
+            if not conds:
+                copy.start()
+            else:
+                pl.when(conds[0] if len(conds) == 1 else jnp.logical_and(*conds))(copy.start)
+
+    feeds = lax.rem(gy, 16) == 15
+    usual = jnp.logical_not(feeds)
+    first = [v if d in URGENT else jnp.logical_and(v, usual) for d, v in enumerate(ready)]
+    after = [jnp.logical_and(v, feeds) for v in ready]
+    send(0, None, first)
     load_c.wait()
     pack(1)
-    pl.semaphore_wait(barrier, 8)
-    for which in range(2):
-        for m in COPIES[which]:
-            for copy in copies[which][m]:
-                copy.start()
+
+    def gone():
+        for d in URGENT[:2]:
+            sent(cor_out_d.at[d - 4], cor_in_d.at[d - 4], send_sem.at[d])
+
+    pl.when(feeds)(gone)
+    for d in range(11):
+        if d not in URGENT:
+            send(0, d, after)
+    send(1, None, ready)
+
+    def answer(d):
+        pl.semaphore_wait(token_sem.at[d], 1)
+        send(0, d, None)
+        send(1, d, None)
+
+    for d in TOKEN_ORDER:
+        pl.when(later[d])(lambda d=d: answer(d))
+
+    def pass_on(k):
+        vias[k].wait_recv()
+        pl.when(high_end)(hops[k][0].start)
+        pl.when(low_end)(hops[k][1].start)
 
     arrived = (set(), set())
 
@@ -335,7 +461,13 @@
 
     towers = (t_even, t_odd)
     inner = WIDE - NEAR
+    waits = jnp.logical_and(at_end, later[2])
+    busy = jnp.logical_and(at_end, jnp.logical_not(later[2]))
+    for k, (which, _) in enumerate(RELAYED):
+        pl.when(at_end if which == 0 else waits)(lambda k=k: pass_on(k))
     for z in range(NZ):
+        for k in PASS_ON.get(z, []):
+            pl.when(busy)(lambda k=k: pass_on(k))
         receive(0, z)
         below, above = towers[(z + 1) % 2], towers[z % 2]
         for lo, hi in spans(WIDE, up8(REACH[z])):
@@ -390,9 +522,18 @@
                 grad_ref[z, rows, :] = own * shrink[z, rows, :]
 
     for which in range(2):
-        for m in COPIES[which]:
-            for copy in copies[which][m]:
-                copy.wait_send()
+        _, _, outs, ins = bufs[which]
+        for d in range(8):
+            part, i = (0, d) if d < 2 else (1, d - 2) if d < 4 else (2, d - 4)
+            args = (outs[part].at[i], ins[part].at[i], send_sem.at[8 * which + d])
+            if which == 0 and d in URGENT[:2]:
+                pl.when(usual)(lambda args=args: sent(*args))
+            else:
+                sent(*args)
+        part = [PLANS[which].row_chunks[c] for w, c in RELAYED if w == which]
+        lo, hi = part[0][0], part[-1][0] + part[-1][1]
+        relay = relays[which].at[lo:hi]
+        pl.when(at_end)(lambda relay=relay, which=which: sent(relay, relay, relay_send.at[which]))
 
 
 def shards(density, cotangent):
@@ -403,8 +544,8 @@
         return out
 
     wide, near = 2 * WIDE + ROWS, 2 * NEAR + ROWS
-    shape = jax.ShapeDtypeStruct(density.shape, F32)
-    return pl.pallas_call(
+    shape = pltpu.VMEM(density.shape, F32)
+    results = pl.pallas_call(
         kernel,
         out_shape=(shape, shape),
         in_specs=[pl.BlockSpec(memory_space=pl.ANY)] * 2,
@@ -419,14 +560,39 @@
             pltpu.VMEM((NZ, 2, near, LANES), F32),
             pltpu.VMEM((NZ, 2, near, LANES), F32),
             pltpu.VMEM((NZ, ROWS, LANES), F32),
+            pltpu.VMEM((DENS.rows, LANES), F32),
+            pltpu.VMEM((COTS.rows, LANES), F32),
             *packed(DENS),
             *packed(COTS),
             pltpu.SemaphoreType.DMA((2,)),
+            pltpu.SemaphoreType.DMA((16,)),
             pltpu.SemaphoreType.DMA((N_SEMS,)),
-            pltpu.SemaphoreType.DMA((N_SEMS,)),
+            pltpu.SemaphoreType.REGULAR((11,)),
+            pltpu.SemaphoreType.DMA((2,)),
+            pltpu.SemaphoreType.DMA((len(RELAYED),)),
         ],
         compiler_params=pltpu.CompilerParams(collective_id=0, has_side_effects=True),
     )(density, cotangent)
+    final = jax.ShapeDtypeStruct(density.shape, F32)
+    return pl.pallas_call(
+        store,
+        out_shape=(final, final),
+        in_specs=[pl.BlockSpec(memory_space=pltpu.VMEM)] * 2,
+        out_specs=(pl.BlockSpec(memory_space=pl.ANY),) * 2,
+        scratch_shapes=[pltpu.SemaphoreType.DMA((8,))],
+    )(*(pltpu.with_memory_space_constraint(v, pltpu.VMEM) for v in results))
+
+
+def store(printed_ref, grad_ref, printed_hbm, grad_hbm, sem):
+    copies = []
+    for i in range(8):
+        src, dst = ((printed_ref, printed_hbm), (grad_ref, grad_hbm))[i % 2]
+        part = slice(4 * (i // 2), 4 * (i // 2) + 4)
+        copies.append(pltpu.make_async_copy(src.at[part], dst.at[part], sem.at[i]))
+    for copy in copies:
+        copy.start()
+    for copy in copies:
+        copy.wait()
 
 
 def solution(mesh):

time: 39.8 us -> 32.2 us (0.81)
  Pallas kernels: 36.3 us -> 31.5 us
  local copies, waits for them, and re-layouts: 2.74 us -> 0 us
    pallas_call x1, Pallas kernels: 36.3 us -> 30.5 us  [shards(): pl.pallas_call(kernel, out_shape=(shape, shape), in_specs=[pl.BlockSpec(m...]
    unnamed x4 -> x0, local copies, waits for them, and re-layouts: 2.74 us -> none
    pallas_call x0 -> x1, Pallas kernels: none -> 1.03 us  [shards(): pl.pallas_call(store, out_shape=(final, final), in_specs=[pl.BlockSpec(me...]
where the time goes in v2:
time: 32.2 us; the launch traced here: 32.1 us
  Pallas kernels  31.5 us (98%)
  between operations  0.64 us (2%)
    pallas_call x1, Pallas kernels, shards(): pl.pallas_call(kernel, out_shape=(shape, shape), in_specs=[pl.BlockSpec(m...  30.5 us
    pallas_call x1, Pallas kernels, shards(): pl.pallas_call(store, out_shape=(final, final), in_specs=[pl.BlockSpec(me...  1.03 us

profile of v2, /device:TPU:8, one launch (start us, length us, event | category | flops | bytes accessed | tf_op | source)
XLA Modules:
  0.0 32.1 jit_solution(13994906799503460064)
XLA Ops:
  0.6 30.5 %shard_map.41 = (f32[16,64,128]{2,1,0:T(8,128)S(1)}, f32[16,64,128]{2,1,0:T(8,128)S(1)}) custom-call(f32[16,64,128]{2,1,0:T(8,128)} %dens_hbm.1, f32[16,64,128]{2,1,0:T(8,128)} %cots_hbm.1), custom_call_target="tpu_custom_call" | custom-call | tf_op jit(solution)/shard_map/pallas_call | solution.py:548
  31.1 1.0 %shard_map.42 = (f32[16,64,128]{2,1,0:T(8,128)}, f32[16,64,128]{2,1,0:T(8,128)}) custom-call(f32[16,64,128]{2,1,0:T(8,128)S(1)} %get-tuple-element.4.printed_ref, f32[16,64,128]{2,1,0:T(8,128)S(1)} %get-tuple-element.5.grad_ref), custom_call_target="tpu_custom_call" | custom-call | tf_op jit(solution)/shard_map/pallas_call | solution.py:577

commit v3 on v2

--- a/solution.py
+++ b/solution.py
@@ -26,14 +26,14 @@
     return (n + 7) // 8 * 8
 
 
-def place(counts):
+def place(counts, tight):
     out, vec, first, last, prev = [], 0, None, 0, 0
     for n in counts:
         if first is None:
             off, first = 0, n
         else:
-            off = last + max(prev, n)
-            if off > LANES - first or off + n > LANES:
+            off = last + (prev if tight else max(prev, n))
+            if off + n > LANES or (off > LANES - first and not tight):
                 vec, off, first = vec + 1, 0, n
         out.append((vec, off))
         last, prev = off, n
@@ -52,7 +52,7 @@
 
 
 class Plan:
-    def __init__(self, order, width, merges):
+    def __init__(self, order, width, merges, groups, tight):
         self.order, self.width = order, width
         self.starts, chunks, self.rows = stream(order, width)
         self.row_chunks, self.row_need, at = [], {}, 0
@@ -62,11 +62,12 @@
                 self.row_need[z] = len(self.row_chunks)
             self.row_chunks.append((part[0][0], sum(n for _, n in part)))
             at += count
-        places, self.col_vecs = place([width(z) for z in order])
+        places, self.col_vecs = place([width(z) for z in order], True)
         self.cols = {z: p for z, p in zip(order, places)}
         self.corners, base = {}, 0
         firsts = []
-        for bands in ((0,), (1,), (2, 3)):
+        self.tight = tight
+        for bands in groups:
             items = [
                 (z, b, width(z) - 8 * b - 1)
                 for b in bands
@@ -75,7 +76,7 @@
             ]
             if not items:
                 continue
-            places, vecs = place([n for _, _, n in items])
+            places, vecs = place([n for _, _, n in items], tight)
             for (z, b, n), (vec, off) in zip(items, places):
                 self.corners[(z, b)] = (base + vec, off, n)
             for vec in range(vecs):
@@ -104,8 +105,8 @@
         return need
 
 
-DENS = Plan(list(range(NZ)), lambda z: REACH[z], [1] * 8 + [2] * 4)
-COTS = Plan(list(range(NZ - 1, 0, -1)), lambda z: z, [1, 1, 2, 4, 7])
+DENS = Plan(list(range(NZ)), lambda z: REACH[z], [1] * 8 + [2] * 4, ((0,), (1,), (2, 3)), False)
+COTS = Plan(list(range(NZ - 1, 0, -1)), lambda z: z, [1, 1, 2, 4, 7], ((0, 1),), True)
 PLANS = (DENS, COTS)
 
 RELAYED = [(0, 8), (0, 9), (0, 10), (0, 11), (1, 0), (1, 1), (1, 2), (1, 3), (1, 4)]
@@ -240,6 +241,7 @@
         slack = 20 if d < 4 else 0 if d < 8 else 30
         if d < 8 and ends[d] is not None:
             slack = slack + (30 - slack) * ends[d].astype(jnp.int32)
+        slack = slack * jnp.minimum(lax.rem(gy + 1, 16), 1) * jnp.minimum(lax.rem(y + 1, 16), 1)
         later.append(lag > slack)
         ready.append(lag <= slack)
         mutual = jnp.logical_and(lag <= slack, lag >= -slack)
@@ -283,12 +285,12 @@
                 if v != vec:
                     continue
                 w = plan.width(z)
-                turned = rotate(src[z, 0, margin : margin + ROWS, :], off)
+                own = src[z, 0, margin : margin + ROWS, :]
                 if low is None:
-                    low = high = turned
+                    low, high = rotate(own, off), rotate(own, off + w)
                 else:
-                    low = jnp.where(lane >= off, turned, low)
-                    high = jnp.where((lane >= off - w) & (lane < off), turned, high)
+                    low = jnp.where(lane >= off, rotate(own, off), low)
+                    high = jnp.where(lane >= off, rotate(own, off + w), high)
             col[0, vec * ROWS : (vec + 1) * ROWS, :] = low
             col[1, vec * ROWS : (vec + 1) * ROWS, :] = high
         lane = lane_ids((8, LANES))
@@ -299,12 +301,15 @@
                     if v != vec:
                         continue
                     lo = margin + 8 * b if side == 0 else margin + ROWS - 8 * (b + 1)
-                    turned = rotate(src[z, 0, lo : lo + 8, :], off)
+                    own = src[z, 0, lo : lo + 8, :]
+                    turned = rotate(own, off)
+                    other = rotate(own, off + n) if plan.tight else turned
+                    start, end = (off, LANES) if plan.tight else (off - n, off)
                     if low is None:
-                        low = high = turned
+                        low, high = turned, other
                     else:
                         low = jnp.where(lane >= off, turned, low)
-                        high = jnp.where((lane >= off - n) & (lane < off), turned, high)
+                        high = jnp.where((lane >= start) & (lane < end), other, high)
                 cor[2 * side, 8 * vec : 8 * vec + 8, :] = low
                 cor[2 * side + 1, 8 * vec : 8 * vec + 8, :] = high
 
@@ -416,13 +421,20 @@
         send(0, d, None)
         send(1, d, None)
 
-    for d in TOKEN_ORDER:
+    for d in TOKEN_ORDER[:-3]:
         pl.when(later[d])(lambda d=d: answer(d))
 
     def pass_on(k):
         vias[k].wait_recv()
         pl.when(high_end)(hops[k][0].start)
         pl.when(low_end)(hops[k][1].start)
+
+    waits = jnp.logical_and(at_end, later[2])
+    busy = jnp.logical_and(at_end, jnp.logical_not(later[2]))
+    for k, (which, _) in enumerate(RELAYED):
+        pl.when(at_end if which == 0 else waits)(lambda k=k: pass_on(k))
+    for d in TOKEN_ORDER[-3:]:
+        pl.when(later[d])(lambda d=d: answer(d))
 
     arrived = (set(), set())
 
@@ -443,28 +455,28 @@
         vec, off = plan.cols[z]
         lane = lane_ids((ROWS, LANES))
         part = slice(vec * ROWS, (vec + 1) * ROWS)
-        both = jnp.where((lane >= off) & (lane < off + w), col[0, part, :], col[1, part, :])
-        dst[z, 1, margin : margin + ROWS, :] = rotate(both, LANES - off)
+        low, high = rotate(col[0, part, :], LANES - off), rotate(col[1, part, :], 2 * LANES - off - w)
+        dst[z, 1, margin : margin + ROWS, :] = jnp.where(lane < LANES // 2, low, high)
         lane = lane_ids((8, LANES))
         for b in range(4):
             if (z, b) not in plan.corners:
                 continue
             vec, off, n = plan.corners[(z, b)]
             part = slice(8 * vec, 8 * vec + 8)
-            slot = (lane >= off) & (lane < off + n)
-            low = jnp.where(slot, cor[0, part, :], cor[1, part, :])
-            high = jnp.where(slot, cor[2, part, :], cor[3, part, :])
+            def merge(i):
+                low, high = cor[i, part, :], cor[i + 1, part, :]
+                if plan.tight:
+                    low, high = rotate(low, LANES - off), rotate(high, 2 * LANES - off - n)
+                    return jnp.where(lane < LANES // 2, low, high)
+                return rotate(jnp.where((lane >= off) & (lane < off + n), low, high), LANES - off)
+
             lo = margin + ROWS + 8 * b
-            dst[z, 1, lo : lo + 8, :] = rotate(low, LANES - off)
+            dst[z, 1, lo : lo + 8, :] = merge(0)
             lo = margin - 8 * (b + 1)
-            dst[z, 1, lo : lo + 8, :] = rotate(high, LANES - off)
+            dst[z, 1, lo : lo + 8, :] = merge(2)
 
     towers = (t_even, t_odd)
     inner = WIDE - NEAR
-    waits = jnp.logical_and(at_end, later[2])
-    busy = jnp.logical_and(at_end, jnp.logical_not(later[2]))
-    for k, (which, _) in enumerate(RELAYED):
-        pl.when(at_end if which == 0 else waits)(lambda k=k: pass_on(k))
     for z in range(NZ):
         for k in PASS_ON.get(z, []):
             pl.when(busy)(lambda k=k: pass_on(k))

time: 32.2 us -> 30.5 us (0.947)
  Pallas kernels: 31.5 us -> 29.7 us
    pallas_call x1, Pallas kernels: 30.5 us -> 28.7 us  [shards(): pl.pallas_call(kernel, out_shape=(shape, shape), in_specs=[pl.BlockSpec(m...]
where the time goes in v3:
time: 30.5 us; the launch traced here: 30.4 us
  Pallas kernels  29.7 us (97%)
  between operations  0.64 us (2%)
    pallas_call x1, Pallas kernels, shards(): pl.pallas_call(kernel, out_shape=(shape, shape), in_specs=[pl.BlockSpec(m...  28.7 us
    pallas_call x1, Pallas kernels, shards(): pl.pallas_call(store, out_shape=(final, final), in_specs=[pl.BlockSpec(me...  1.03 us

profile of v3, /device:TPU:8, one launch (start us, length us, event | category | flops | bytes accessed | tf_op | source)
XLA Modules:
  0.0 30.4 jit_solution(18089076510239593246)
XLA Ops:
  0.6 28.7 %shard_map.41 = (f32[16,64,128]{2,1,0:T(8,128)S(1)}, f32[16,64,128]{2,1,0:T(8,128)S(1)}) custom-call(f32[16,64,128]{2,1,0:T(8,128)} %dens_hbm.1, f32[16,64,128]{2,1,0:T(8,128)} %cots_hbm.1), custom_call_target="tpu_custom_call" | custom-call | tf_op jit(solution)/shard_map/pallas_call | solution.py:560
  29.4 1.0 %shard_map.42 = (f32[16,64,128]{2,1,0:T(8,128)}, f32[16,64,128]{2,1,0:T(8,128)}) custom-call(f32[16,64,128]{2,1,0:T(8,128)S(1)} %get-tuple-element.4.printed_ref, f32[16,64,128]{2,1,0:T(8,128)S(1)} %get-tuple-element.5.grad_ref), custom_call_target="tpu_custom_call" | custom-call | tf_op jit(solution)/shard_map/pallas_call | solution.py:589

commit v4 on v3

--- a/solution.py
+++ b/solution.py
@@ -1,3 +1,4 @@
+import functools
 import math
 
 import jax
@@ -139,10 +140,11 @@
 def rank(gx, gy):
     x, y = lax.rem(gx, 4), 2 * lax.div(gx, 4) + lax.div(gy, 16)
     z, core = lax.rem(lax.div(gy, 2), 8), lax.rem(gy, 2)
-    far = lax.div(y, 4)
-    hops = y * (1 - 2 * far) + 8 * far
+    far, deep = lax.div(y, 4), lax.div(z, 4)
+    along_y = 6 * y * (1 - far) + (15 + 3 * (8 - y)) * far
+    along_z = 13 * z * (1 - deep) + (41 + 5 * z) * deep
     first = 1 - lax.div(gx * 32 + gy + 511, 512)
-    return 13 * z + 8 * hops + 9 * x + 4 * (1 - core) + 60 * first
+    return along_z + along_y + 4 * x + 6 * (1 - core) + 60 * first
 
 
 def lane_ids(shape):
@@ -400,8 +402,24 @@
 
     feeds = lax.rem(gy, 16) == 15
     usual = jnp.logical_not(feeds)
-    first = [v if d in URGENT else jnp.logical_and(v, usual) for d, v in enumerate(ready)]
-    after = [jnp.logical_and(v, feeds) for v in ready]
+    holds = jnp.logical_and(at_end, lax.rem(lax.div(gy, 2), 8) == 7)
+    freed = jnp.logical_not(holds)
+    held = {}
+    for d, end in enumerate(ends):
+        if end is not None:
+            held[d] = jnp.logical_and(end, holds)
+            if d in URGENT:
+                held[d] = jnp.logical_and(held[d], usual)
+
+    def gated(gate, *more):
+        return functools.reduce(jnp.logical_and, more, gate)
+
+    first, after, last = [], [], []
+    for d, v in enumerate(ready):
+        loose = (jnp.logical_not(held[d]),) if d in held else ()
+        first.append(gated(v, *loose) if d in URGENT else gated(v, usual, *loose))
+        after.append(gated(v, feeds, *loose))
+        last.append(gated(v, held[d]) if d in held else None)
     send(0, None, first)
     load_c.wait()
     pack(1)
@@ -414,6 +432,14 @@
     for d in range(11):
         if d not in URGENT:
             send(0, d, after)
+
+    def columns():
+        for c in range(DENS.col_vecs):
+            copies[0][("col", c)][1].wait_recv()
+
+    pl.when(holds)(columns)
+    for d in held:
+        send(0, d, last)
     send(1, None, ready)
 
     def answer(d):
@@ -447,8 +473,11 @@
         for m in wanted:
             if m not in arrived[which]:
                 arrived[which].add(m)
-                for copy in copies[which][m]:
-                    copy.wait_recv()
+                for i, copy in enumerate(copies[which][m]):
+                    if which == 0 and m[0] == "col" and i == 1:
+                        pl.when(freed)(copy.wait_recv)
+                    else:
+                        copy.wait_recv()
         w, at = plan.width(z), plan.starts[z]
         dst[z, 0, margin + ROWS : margin + ROWS + w, :] = row[0, at : at + w, :]
         dst[z, 0, margin - w : margin, :] = row[1, at : at + w, :]

time: 30.5 us -> 29.9 us (0.980)
  Pallas kernels: 29.7 us -> 29.2 us
    pallas_call x1, Pallas kernels: 28.7 us -> 28.1 us  [shards(): pl.pallas_call(kernel, out_shape=(shape, shape), in_specs=[pl.BlockSpec(m...]
where the time goes in v4:
time: 29.9 us; the launch traced here: 29.8 us
  Pallas kernels  29.2 us (98%)
  between operations  0.64 us (2%)
    pallas_call x1, Pallas kernels, shards(): pl.pallas_call(kernel, out_shape=(shape, shape), in_specs=[pl.BlockSpec(m...  28.1 us
    pallas_call x1, Pallas kernels, shards(): pl.pallas_call(store, out_shape=(final, final), in_specs=[pl.BlockSpec(me...  1.03 us

profile of v4, /device:TPU:8, one launch (start us, length us, event | category | flops | bytes accessed | tf_op | source)
XLA Modules:
  0.0 29.8 jit_solution(4560694196350602819)
XLA Ops:
  0.6 28.1 %shard_map.41 = (f32[16,64,128]{2,1,0:T(8,128)S(1)}, f32[16,64,128]{2,1,0:T(8,128)S(1)}) custom-call(f32[16,64,128]{2,1,0:T(8,128)} %dens_hbm.1, f32[16,64,128]{2,1,0:T(8,128)} %cots_hbm.1), custom_call_target="tpu_custom_call" | custom-call | tf_op jit(solution)/shard_map/pallas_call | solution.py:589
  28.8 1.0 %shard_map.42 = (f32[16,64,128]{2,1,0:T(8,128)}, f32[16,64,128]{2,1,0:T(8,128)}) custom-call(f32[16,64,128]{2,1,0:T(8,128)S(1)} %get-tuple-element.4.printed_ref, f32[16,64,128]{2,1,0:T(8,128)S(1)} %get-tuple-element.5.grad_ref), custom_call_target="tpu_custom_call" | custom-call | tf_op jit(solution)/shard_map/pallas_call | solution.py:618
